TPU v7x, 32 devices: a whole 2x2x4 slice. The times are simulated.
32 devices in a mesh: groups: 2 (over x), kv: 16 (over z, y, core).
Axes of the slice: x: 2, y: 2, z: 4, core: 2. Of those that a mesh axis runs over, the one named last changes fastest.
Arguments:
- queries: bfloat16 [80, 18432], P('groups', 'kv'), parts along dimension 0, may hold values from -240 to 240
- latent_cache: bfloat16 [80, 2048, 576], P('groups', 'kv'), parts along dimension 0, may hold values from -6 to 6
- context_lengths: int32 [80], P('groups'), parts along dimension 0, may hold values from 128 to 2048, as said below
- value_up: bfloat16 [16384, 128], P('kv'), may hold values from -0.25 to 0.25
- out_proj: bfloat16 [4096, 7168], P('kv'), may hold values from -0.09375 to 0.09375
- residual: bfloat16 [80, 7168], P('groups', 'kv'), parts along dimension 0, may hold values from -0.75 to 0.75
- norm_gain: bfloat16 [7168], P('kv'), may hold values from 0.5 to 1.5
- expert_ids: int32 [80, 8], P('groups'), parts along dimension 0, may hold values from 0 to 255, all different within a row; in each aligned block of 40 rows (0 to 39, 40 to 79, ...) at most 2 rows name the same one
- gate_weights: float32 [80, 8], P('groups'), parts along dimension 0, may hold values from 0.05 to 0.5
Outputs:
- dispatched: bfloat16 [512, 2, 7168], P(('groups', 'kv')), parts along dimension 0
- slot_scale: float32 [512, 2], P(('groups', 'kv')), parts along dimension 0
- slot_gate: float32 [512, 2], P(('groups', 'kv')), parts along dimension 0
There are 2 independent parts, one for each index of `groups`. A program takes and returns all parts, laid end to end along the dimension named above; an argument that names none is the same for every part. Nothing has to cross between parts.
Inputs may be any that keep to these rules, and one draw needn't show every extreme that they name: `context_lengths`: multiples of 128; some sequence is 2048 long. `expert_ids`: each token names 8 different experts; no expert is named by more than 2 tokens, a bound that some block reaches.
All inputs are finite; a program needn't handle non-finite values. Where the computation divides by a largest or mean magnitude, that divisor is 1e-20 or more.
Results may differ from a plain program's by a relative error of at most 0.0069.
Values may be sent and summed in bfloat16 or wider, within the bound.
A program may use at most 64 MiB of HBM per device.

v0:
```python
import jax
import jax.numpy as jnp
from jax import lax
from jax.sharding import PartitionSpec as P

H = 32
LAT = 512
ROPE = 64
VD = 128
D = 7168
EXPERTS = 256
TOPK = 8
CAP = 2
score_scale = 192.0 ** (-0.5)
masked_score = -1e30
small_eps = 1e-06


def from_partner(value, axis, bit):
    mask = 2**bit
    pairs = [(source, source ^ mask) for source in range(lax.axis_size(axis))]
    return lax.ppermute(value, axis, pairs)


def slot_targets(expert_ids):
    flat_ids = expert_ids.reshape(-1)
    order_index = jnp.arange(flat_ids.shape[0], dtype=jnp.int32)
    same_before = (flat_ids[:, None] == flat_ids[None, :]) & (
        order_index[None, :] < order_index[:, None]
    )
    rank_within = jnp.sum(same_before.astype(jnp.int32), axis=1)
    return flat_ids * CAP + rank_within


def slot_match(targets, first_slot, slot_count):
    slot_index = first_slot + jnp.arange(slot_count, dtype=jnp.int32)
    return (slot_index[:, None] == targets[None, :]).astype(jnp.float32)


def token_picker(matches, seq_count):
    return jnp.sum(matches.reshape(matches.shape[0], seq_count, TOPK), axis=2)


def per_device(
    queries,
    latent_cache,
    context_lengths,
    value_up,
    out_proj,
    residual,
    norm_gain,
    expert_ids,
    gate_weights,
):
    kv_count = lax.axis_size("kv")
    shard_index = lax.axis_index("kv")
    seq_count = queries.shape[0]
    query_rows = lax.all_gather(queries, "kv", axis=1, tiled=True).reshape(seq_count, H, LAT + ROPE)
    ctx_local = latent_cache.shape[1]
    scores = (
        jnp.einsum("shq,scq->shc", query_rows, latent_cache, preferred_element_type=jnp.float32)
        * score_scale
    )
    position = shard_index * ctx_local + jnp.arange(ctx_local, dtype=jnp.int32)
    valid_mask = (position[None, :] < context_lengths[:, None])[:, None, :]
    scores = jnp.where(valid_mask, scores, masked_score)
    local_max = jnp.max(scores, axis=2)
    weights = jnp.where(valid_mask, jnp.exp(scores - local_max[:, :, None]), 0.0)
    local_total = jnp.sum(weights, axis=2)
    local_out = jnp.einsum(
        "shc,scl->shl",
        weights.astype(jnp.bfloat16),
        latent_cache[:, :, :LAT],
        preferred_element_type=jnp.float32,
    )
    out_rows = out_proj.shape[0]
    col_count = H * LAT // kv_count
    segment = min(col_count, LAT)
    head_count = col_count // segment
    head_start = shard_index * col_count // LAT
    global_max = lax.pmax(local_max, "kv")
    scaling = jnp.exp(local_max - global_max)
    weight_total = lax.psum(local_total * scaling, "kv")
    scaled = (local_out * scaling[:, :, None]).reshape(seq_count, H * LAT)
    merged_sum = lax.psum_scatter(scaled, "kv", scatter_dimension=1, tiled=True).reshape(
        seq_count, head_count, segment
    )
    own_total = lax.dynamic_slice_in_dim(weight_total, head_start, head_count, 1)
    merged = merged_sum / own_total[:, :, None]
    projector = value_up.reshape(head_count, segment, VD).astype(jnp.float32)
    value_part = jnp.einsum("shl,hlv->shv", merged, projector, precision=lax.Precision.HIGHEST)
    holders = kv_count // H if kv_count > H else 1
    for bit in range(holders.bit_length() - 1):
        value_part = value_part + from_partner(value_part, "kv", bit)
    value_rows = value_part.astype(jnp.bfloat16).reshape(seq_count, head_count * VD)
    if holders > 1:
        value_rows = lax.dynamic_slice_in_dim(
            value_rows, shard_index % holders * out_rows, out_rows, 1
        )
    partial_out = jnp.dot(value_rows, out_proj, preferred_element_type=jnp.float32)
    experts_local = EXPERTS // kv_count
    slot_count = experts_local * CAP
    targets = slot_targets(expert_ids)
    own_match = slot_match(targets, shard_index * slot_count, slot_count)
    own_pick = token_picker(own_match, seq_count)
    slot_gate = jnp.dot(own_match, gate_weights.reshape(-1), precision=lax.Precision.HIGHEST)
    attn_rows = lax.psum(partial_out, "kv")
    resid_rows, gain_cols = (
        lax.all_gather(residual, "kv", axis=1, tiled=True),
        lax.all_gather(norm_gain, "kv", axis=0, tiled=True),
    )
    summed = attn_rows + resid_rows.astype(jnp.float32)
    inverse_rms = lax.rsqrt(jnp.mean(summed * summed, axis=1) + small_eps)
    normed = summed * inverse_rms[:, None] * gain_cols.astype(jnp.float32)
    peak_abs = jnp.max(jnp.abs(normed), axis=1) + small_eps
    coded_rows = (normed / peak_abs[:, None]).astype(jnp.bfloat16)
    dispatched = jnp.dot(
        own_pick.astype(jnp.bfloat16), coded_rows, preferred_element_type=jnp.float32
    ).astype(jnp.bfloat16)
    slot_scale = jnp.dot(own_pick, peak_abs, precision=lax.Precision.HIGHEST)
    return (
        dispatched.reshape(experts_local, CAP, D),
        slot_scale.reshape(experts_local, CAP),
        slot_gate.reshape(experts_local, CAP),
    )


def solution(mesh):
    in_specs = (
        P("groups", "kv"),
        P("groups", "kv", None),
        P("groups"),
        P("kv", None),
        P("kv", None),
        P("groups", "kv"),
        P("kv"),
        P("groups", None),
        P("groups", None),
    )
    out_specs = (
        P(("groups", "kv"), None, None),
        P(("groups", "kv"), None),
        P(("groups", "kv"), None),
    )
    return jax.shard_map(
        per_device, mesh=mesh, in_specs=in_specs, out_specs=out_specs, check_vma=False
    )
```

profile of v0, /device:TPU:0, one launch (start us, length us, event | category | flops | bytes accessed | tf_op | source)
XLA Modules:
  0.0 314.2 jit_solution(11004834008479304627)
XLA Ops:
  7.2 0.0 copy-start
  7.2 0.0 all-gather.3.cloned.1.call-start
  7.2 0.7 all-gather.3.cloned.1.call-update
  7.9 0.0 reduce-scatter.2.cloned.1.call-start
  8.0 0.7 broadcast_compare_fusion.1
  8.7 43.6 %all-gather.3.cloned.1.call-done = bf16[40,18432]{1,0:T(8,128)(2,1)} async-done(((bf16[40,1152]{1,0:T(8,128)(2,1)}), bf16[40,18432]{1,0:T(8,128)(2,1)}) %all-gather.3.cloned.1.call-update) | async-done | bytes 1474576 | tf_op jit(solution)/shard_map/all_gather | solution.py:58
  52.3 3.3 %reshape.111 = bf16[40,32,576]{2,1,0:T(8,128)(2,1)S(1)} reshape(bf16[40,18432]{1,0:T(8,128)(2,1)} %all-gather.3.cloned.1.call-done) | data formatting | bytes 2949120 | tf_op jit(solution)/shard_map/reshape | solution.py:58
  55.5 3.9 %fusion.26 = (f32[40,32]{1,0:T(8,128)S(1)}, f32[40,32,128]{2,1,0:T(8,128)S(1)}) fusion(bf16[40,32,576]{2,1,0:T(8,128)(2,1)S(1)} %reshape.111, bf16[40,128,576]{1,2,0:T(8,128)(2,1)} %param.10, pred[40,128]{1,0:T(8,128)(4,1)S(1)} %broadcast_compare_fusion.1), kind=kOutput, calls=%fused_computation.47 | convolution fusion | flops 189233920 | bytes 8038400 | tf_op jit(solution)/shard_map/shq,scq->shc/dot_general | solution.py:61
  59.4 59.5 %pmax.7 = f32[40,32]{1,0:T(8,128)S(1)} all-reduce(f32[40,32]{1,0:T(8,128)S(1)} %get-tuple-element.5), channel_id=1, replica_groups=mesh['groups'=2,'kv'=16] {'kv'}, use_global_device_ids=true, to_apply=%region_3.4 | all-reduce | flops 1280 | bytes 10240 | tf_op jit(solution)/shard_map/pmax | solution.py:81
  118.9 0.4 fusion.7
  119.4 3.9 %fusion.2 = f32[40,32,512]{2,1,0:T(8,128)S(1)} fusion(bf16[40,128,576]{1,2,0:T(8,128)(2,1)} %param.10, f32[40,32]{1,0:T(8,128)S(1)} %get-tuple-element.4, f32[40,32,128]{2,1,0:T(8,128)S(1)} %get-tuple-element.6, f32[40,32]{1,0:T(8,128)S(1)} %get-tuple-element.5, pred[40,128]{1,0:T(8,128)(4,1)S(1)} %broadcast_compare_fusion.1), kind=kOutput, calls=%fused_computation.3 | convolution fusion | flops 168919040 | bytes 8535040 | tf_op jit(solution)/shard_map/shc,scl->shl/dot_general | solution.py:70
  123.3 3.0 copy.51
  126.3 0.0 copy-start.3
  126.3 0.0 copy-start.2
  126.3 0.0 reduce-scatter.2.cloned.1.call-update
  126.3 0.0 all-reduce.3.cloned.1.call-start
  126.4 0.6 copy-done.3
  127.0 0.1 copy.38
  127.1 0.1 eq.41
  127.2 0.2 convert_reduce_fusion
  127.4 0.1 reduce_sum.39
  127.5 0.1 copy.39
  127.6 0.0 copy-done.2
  127.6 19.1 %all-gather = bf16[16,448,40]{1,2,0:T(8,128)(2,1)S(1)} all-gather(bf16[1,448,40]{1,2,0:T(8,128)(2,1)S(1)} %bitcast.43), channel_id=1, replica_groups=mesh['groups'=2,'kv'=16] {'kv'}, dimensions={0}, use_global_device_ids=true | all-gather | bytes 609280 | tf_op jit(solution)/shard_map/all_gather | solution.py:109
  146.7 59.9 %psum.14 = f32[40,32]{1,0:T(8,128)S(1)} all-reduce(f32[40,32]{1,0:T(8,128)S(1)} %get-tuple-element.3), channel_id=1, replica_groups=mesh['groups'=2,'kv'=16] {'kv'}, use_global_device_ids=true, to_apply=%region_6.7 | all-reduce | flops 1280 | bytes 10240 | tf_op jit(solution)/shard_map/psum | solution.py:83
  206.7 0.1 constant_dynamic-slice_fusion
  206.7 0.0 reduce-scatter.2.cloned.1.call-done
  206.7 1.1 reshape.113
  207.8 0.1 broadcast_divide_fusion
  207.9 0.0 copy-done
  207.9 0.2 fusion.6
  208.2 3.8 %fusion.17 = f32[40,7168]{1,0:T(8,128)} fusion(bf16[256,7168]{1,0:T(8,128)(2,1)} %param.13, bf16[2,5,8,128]{3,2,1,0:T(8,128)(2,1)S(1)} %fusion.6), kind=kOutput, calls=%fused_computation.28 | convolution fusion | flops 146800640 | bytes 4837376 | tf_op jit(solution)/shard_map/dot_general | solution.py:100
  212.0 0.0 all-reduce.3.cloned.1.call-update
  212.1 0.2 copy.43
  212.3 0.0 copy-start.6
  212.3 0.0 copy-start.5
  212.3 0.0 copy-start.4
  212.3 0.5 reshape.125
  212.9 0.1 copy-done.6
  212.9 0.6 dynamic-slice
  214.2 0.0 copy-done.5
  214.2 0.3 dynamic-update-slice
  214.4 57.8 %all-reduce = bf16[7168]{0:T(1024)(128)(2,1)S(1)} all-reduce(bf16[7168]{0:T(1024)(128)(2,1)S(1)} %dynamic-update-slice), channel_id=1, replica_groups=mesh['groups'=2,'kv'=16] {'kv'}, use_global_device_ids=true, to_apply=%add | all-reduce | flops 7168 | bytes 28672
  272.3 0.0 copy-done.4
  272.3 0.1 copy.44
  272.3 0.1 reshape.128
  272.4 0.1 convert_reduce_fusion.1
  272.6 0.1 broadcast_compare_fusion
  272.7 0.8 fusion.15
  273.5 30.1 %all-reduce.3.cloned.1.call-done = f32[40,7168]{1,0:T(8,128)} async-done(((f32[40,7168]{1,0:T(8,128)}), f32[40,7168]{1,0:T(8,128)}) %all-reduce.3.cloned.1.call-update) | async-done | bytes 1146896 | tf_op jit(solution)/shard_map/psum | solution.py:107
  303.6 0.0 copy-start.1
  303.6 1.6 multiply_reduce_fusion
  305.1 0.0 copy-done.1
  305.2 0.4 abs_reduce_fusion
  305.5 0.4 convolution_convert_fusion
  306.0 0.9 reshape.116
  306.9 0.8 fusion.20
  (10 shorter events, 0.1 us)
Async XLA Ops:
  7.2 200.8 %copy-start = (bf16[1024,128]{1,0:T(8,128)(2,1)S(1)}, bf16[1024,128]{1,0:T(8,128)(2,1)}, u32[]{:S(2)}) copy-start(bf16[1024,128]{1,0:T(8,128)(2,1)} %param.12) | copy-start | bytes 786436
  7.2 45.1 %all-gather.3.cloned.1.call-start = ((), (), s32[]{:S(2)}) async-start(), calls=%async_computation.1 | async-start | bytes 1566720 | tf_op jit(solution)/shard_map/all_gather | solution.py:58
  7.9 198.8 %reduce-scatter.2.cloned.1.call-start = ((), (), s32[]{:S(2)}) async-start(), calls=%async_computation.2 | async-start | bytes 2785280 | tf_op jit(solution)/shard_map/reduce_scatter | solution.py:85
  126.3 0.7 copy-start.3
  126.3 1.3 copy-start.2
  126.3 177.2 %all-reduce.3.cloned.1.call-start = ((), (), s32[]{:S(2)}) async-start(), calls=%async_computation.3 | async-start | bytes 2293760 | tf_op jit(solution)/shard_map/psum | solution.py:107
  212.3 0.7 copy-start.6
  212.3 1.9 copy-start.5
  212.3 60.0 %copy-start.4 = (f32[40,8]{0,1:T(8,128)S(1)}, f32[40,8]{0,1:T(8,128)}, u32[]{:S(2)}) copy-start(f32[40,8]{0,1:T(8,128)} %param.17) | copy-start | bytes 3844
  303.6 1.6 copy-start.1
Sparse Core Ops, SparseCore 0:
  10.2 42.0 all-gather.2
  126.5 61.4 reduce-scatter.1
  212.2 91.3 all-reduce.2
where the time goes:
time: 315 us; the launch traced here: 314 us
  blocking collectives  196 us (62%)
  waiting for transfers between devices  74.4 us (24%)
  between operations  14.6 us (5%)
  matrix products  13.9 us (4%)
  local copies, waits for them, and re-layouts  11.1 us (4%)
  other arithmetic  3.74 us (1%)
    psum x1, blocking collectives, per_device(): weight_total = lax.psum(local_total * scaling, 'kv')  59.9 us
    pmax x1, blocking collectives, per_device(): global_max = lax.pmax(local_max, 'kv')  59.5 us
    unnamed x1, blocking collectives  57.8 us
    all_gather x1, waiting for transfers between devices, per_device(): lax.all_gather(queries, 'kv', axis=1, tiled=True)  43.6 us
    psum x1, waiting for transfers between devices, per_device(): attn_rows = lax.psum(partial_out, 'kv')  30.1 us
    all_gather x1, blocking collectives, per_device(): lax.all_gather(residual, 'kv', axis=1, tiled=True)  19.1 us
  transfers between devices with their start and end apart: 3, of which 2 were waited for; matrix products, arithmetic and copies ran while one was open for 1% of the time, Pallas kernels for 0%

commit v1 on v0

--- a/solution.py
+++ b/solution.py
@@ -80,7 +80,7 @@
     head_start = shard_index * col_count // LAT
     global_max = lax.pmax(local_max, "kv")
     scaling = jnp.exp(local_max - global_max)
-    weight_total = lax.psum(local_total * scaling, "kv")
+    weight_total = jnp.sum(lax.all_gather(local_total * scaling, "kv"), axis=0)
     scaled = (local_out * scaling[:, :, None]).reshape(seq_count, H * LAT)
     merged_sum = lax.psum_scatter(scaled, "kv", scatter_dimension=1, tiled=True).reshape(
         seq_count, head_count, segment

time: 315 us -> 299 us (0.949)
  blocking collectives: 196 us -> 157 us
  waiting for transfers between devices: 74.4 us -> 97.8 us
    psum x1 -> x0, blocking collectives: 59.9 us -> none  [per_device(): weight_total = lax.psum(local_total * scaling, 'kv')]
    reduce_scatter x1, waiting for transfers between devices: 0.01 us -> 22.3 us  [per_device(): lax.psum_scatter(scaled, 'kv', scatter_dimension=1, tiled=True)]
    all_gather x0 -> x1, blocking collectives: none -> 20 us  [per_device(): weight_total = jnp.sum(lax.all_gather(local_total * scaling, 'kv'), axis=0)]
  transfers between devices with their start and end apart: 3 -> 3, of which waited for: 2 -> 3; matrix products, arithmetic and copies ran while one was open for 1% -> 1% of each run, Pallas kernels for 0% -> 0%
where the time goes in v1:
time: 299 us; the launch traced here: 298 us
  blocking collectives  157 us (53%)
  waiting for transfers between devices  97.8 us (33%)
  between operations  14.6 us (5%)
  matrix products  13.9 us (5%)
  local copies, waits for them, and re-layouts  11.2 us (4%)
  other arithmetic  3.76 us (1%)
    pmax x1, blocking collectives, per_device(): global_max = lax.pmax(local_max, 'kv')  59.5 us
    unnamed x1, blocking collectives  58.2 us
    all_gather x1, waiting for transfers between devices, per_device(): lax.all_gather(queries, 'kv', axis=1, tiled=True)  43.6 us
    psum x1, waiting for transfers between devices, per_device(): attn_rows = lax.psum(partial_out, 'kv')  31.2 us
    reduce_scatter x1, waiting for transfers between devices, per_device(): lax.psum_scatter(scaled, 'kv', scatter_dimension=1, tiled=True)  22.3 us
    all_gather x1, blocking collectives, per_device(): weight_total = jnp.sum(lax.all_gather(local_total * scaling, 'kv'), axis=0)  20 us
    all_gather x1, blocking collectives, per_device(): lax.all_gather(residual, 'kv', axis=1, tiled=True)  19.1 us
  transfers between devices with their start and end apart: 3, of which 3 were waited for; matrix products, arithmetic and copies ran while one was open for 1% of the time, Pallas kernels for 0%

profile of v1, /device:TPU:0, one launch (start us, length us, event | category | flops | bytes accessed | tf_op | source)
XLA Modules:
  0.0 298.3 jit_solution(17798542982016087512)
XLA Ops:
  7.2 0.0 copy-start
  7.2 0.0 all-gather.5.cloned.1.call-start
  7.2 0.7 all-gather.5.cloned.1.call-update
  7.9 0.0 reduce-scatter.2.cloned.1.call-start
  8.0 0.7 broadcast_compare_fusion.1
  8.7 43.6 %all-gather.5.cloned.1.call-done = bf16[40,18432]{1,0:T(8,128)(2,1)} async-done(((bf16[40,1152]{1,0:T(8,128)(2,1)}), bf16[40,18432]{1,0:T(8,128)(2,1)}) %all-gather.5.cloned.1.call-update) | async-done | bytes 1474576 | tf_op jit(solution)/shard_map/all_gather | solution.py:58
  52.3 3.3 %reshape.111 = bf16[40,32,576]{2,1,0:T(8,128)(2,1)S(1)} reshape(bf16[40,18432]{1,0:T(8,128)(2,1)} %all-gather.5.cloned.1.call-done) | data formatting | bytes 2949120 | tf_op jit(solution)/shard_map/reshape | solution.py:58
  55.5 3.9 %fusion.25 = (f32[40,32]{1,0:T(8,128)S(1)}, f32[40,32,128]{2,1,0:T(8,128)S(1)}) fusion(bf16[40,32,576]{2,1,0:T(8,128)(2,1)S(1)} %reshape.111, bf16[40,128,576]{1,2,0:T(8,128)(2,1)} %param.10, pred[40,128]{1,0:T(8,128)(4,1)S(1)} %broadcast_compare_fusion.1), kind=kOutput, calls=%fused_computation.47 | convolution fusion | flops 189233920 | bytes 8038400 | tf_op jit(solution)/shard_map/shq,scq->shc/dot_general | solution.py:61
  59.4 59.5 %pmax.7 = f32[40,32]{1,0:T(8,128)S(1)} all-reduce(f32[40,32]{1,0:T(8,128)S(1)} %get-tuple-element.5), channel_id=1, replica_groups=mesh['groups'=2,'kv'=16] {'kv'}, use_global_device_ids=true, to_apply=%region_3.4 | all-reduce | flops 1280 | bytes 10240 | tf_op jit(solution)/shard_map/pmax | solution.py:81
  118.9 0.4 fusion.7
  119.4 3.9 %fusion.2 = f32[40,32,512]{2,1,0:T(8,128)S(1)} fusion(bf16[40,128,576]{1,2,0:T(8,128)(2,1)} %param.10, f32[40,32]{1,0:T(8,128)S(1)} %get-tuple-element.4, f32[40,32,128]{2,1,0:T(8,128)S(1)} %get-tuple-element.6, f32[40,32]{1,0:T(8,128)S(1)} %get-tuple-element.5, pred[40,128]{1,0:T(8,128)(4,1)S(1)} %broadcast_compare_fusion.1), kind=kOutput, calls=%fused_computation.3 | convolution fusion | flops 168919040 | bytes 8535040 | tf_op jit(solution)/shard_map/shc,scl->shl/dot_general | solution.py:70
  123.3 3.0 %copy.65 = f32[5,8,32,512]{3,1,2,0:T(8,128)} copy(f32[5,8,32,512]{3,2,1,0:T(8,128)S(1)} %bitcast.42) | data formatting | bytes 5242880
  126.3 0.0 copy-start.3
  126.3 0.0 copy-start.2
  126.3 0.0 reduce-scatter.2.cloned.1.call-update
  126.3 0.0 all-reduce.3.cloned.1.call-start
  126.4 0.6 copy-done.3
  127.0 0.1 copy.50
  127.1 0.1 eq.41
  127.2 0.2 convert_reduce_fusion
  127.4 0.1 reduce_sum.48
  127.5 0.1 copy.51
  127.6 0.0 copy-done.2
  127.6 19.1 %all-gather.2 = bf16[16,448,40]{1,2,0:T(8,128)(2,1)S(1)} all-gather(bf16[1,448,40]{1,2,0:T(8,128)(2,1)S(1)} %bitcast.45), channel_id=1, replica_groups=mesh['groups'=2,'kv'=16] {'kv'}, dimensions={0}, use_global_device_ids=true | all-gather | bytes 609280 | tf_op jit(solution)/shard_map/all_gather | solution.py:109
  146.7 0.1 copy.53
  146.8 20.0 %all-gather.1 = f32[16,40,32]{1,2,0:T(8,128)S(1)} all-gather(f32[1,40,32]{1,2,0:T(8,128)S(1)} %copy.53), channel_id=2, replica_groups=mesh['groups'=2,'kv'=16] {'kv'}, dimensions={0}, use_global_device_ids=true | all-gather | bytes 87040 | tf_op jit(solution)/shard_map/all_gather | solution.py:83
  166.9 0.1 copy.54
  166.9 22.3 %reduce-scatter.2.cloned.1.call-done = f32[40,1024]{1,0:T(8,128)} async-done(((f32[40,16384]{1,0:T(8,128)}), f32[40,1024]{1,0:T(8,128)}) %reduce-scatter.2.cloned.1.call-update) | async-done | bytes 163856 | tf_op jit(solution)/shard_map/reduce_scatter | solution.py:85
  189.2 1.1 reshape.113
  190.3 0.1 broadcast_divide_fusion
  190.4 0.0 copy-done
  190.4 0.2 fusion.6
  190.7 3.8 %fusion.17 = f32[40,7168]{1,0:T(8,128)} fusion(bf16[256,7168]{1,0:T(8,128)(2,1)} %param.13, bf16[2,5,8,128]{3,2,1,0:T(8,128)(2,1)S(1)} %fusion.6), kind=kOutput, calls=%fused_computation.28 | convolution fusion | flops 146800640 | bytes 4837376 | tf_op jit(solution)/shard_map/dot_general | solution.py:100
  194.5 0.0 all-reduce.3.cloned.1.call-update
  194.6 0.2 copy.57
  194.8 0.0 copy-start.6
  194.8 0.0 copy-start.5
  194.8 0.0 copy-start.4
  194.8 0.5 reshape.129
  195.4 0.1 copy-done.6
  195.4 0.6 dynamic-slice
  196.7 0.0 copy-done.5
  196.7 0.3 dynamic-update-slice
  197.0 58.2 %all-reduce = bf16[7168]{0:T(1024)(128)(2,1)S(1)} all-reduce(bf16[7168]{0:T(1024)(128)(2,1)S(1)} %dynamic-update-slice), channel_id=1, replica_groups=mesh['groups'=2,'kv'=16] {'kv'}, use_global_device_ids=true, to_apply=%add | all-reduce | flops 7168 | bytes 28672
  255.2 0.0 copy-done.4
  255.2 0.1 copy.58
  255.3 0.1 reshape.132
  255.4 0.1 convert_reduce_fusion.1
  255.5 0.1 broadcast_compare_fusion
  255.6 0.8 fusion.15
  256.4 31.2 %all-reduce.3.cloned.1.call-done = f32[40,7168]{1,0:T(8,128)} async-done(((f32[40,7168]{1,0:T(8,128)}), f32[40,7168]{1,0:T(8,128)}) %all-reduce.3.cloned.1.call-update) | async-done | bytes 1146896 | tf_op jit(solution)/shard_map/psum | solution.py:107
  287.6 0.0 copy-start.1
  287.6 1.6 multiply_reduce_fusion
  289.2 0.0 copy-done.1
  289.2 0.4 abs_reduce_fusion
  289.6 0.4 convolution_convert_fusion
  290.0 0.9 reshape.116
  291.0 0.8 fusion.20
  (12 shorter events, 0.1 us)
Async XLA Ops:
  7.2 183.3 %copy-start = (bf16[1024,128]{1,0:T(8,128)(2,1)S(1)}, bf16[1024,128]{1,0:T(8,128)(2,1)}, u32[]{:S(2)}) copy-start(bf16[1024,128]{1,0:T(8,128)(2,1)} %param.12) | copy-start | bytes 786436
  7.2 45.1 %all-gather.5.cloned.1.call-start = ((), (), s32[]{:S(2)}) async-start(), calls=%async_computation.1 | async-start | bytes 1566720 | tf_op jit(solution)/shard_map/all_gather | solution.py:58
  7.9 181.3 %reduce-scatter.2.cloned.1.call-start = ((), (), s32[]{:S(2)}) async-start(), calls=%async_computation.2 | async-start | bytes 2785280 | tf_op jit(solution)/shard_map/reduce_scatter | solution.py:85
  126.3 0.7 copy-start.3
  126.3 1.3 copy-start.2
  126.3 161.3 %all-reduce.3.cloned.1.call-start = ((), (), s32[]{:S(2)}) async-start(), calls=%async_computation.3 | async-start | bytes 2293760 | tf_op jit(solution)/shard_map/psum | solution.py:107
  194.8 0.7 copy-start.6
  194.8 1.9 copy-start.5
  194.8 60.4 %copy-start.4 = (f32[40,8]{0,1:T(8,128)S(1)}, f32[40,8]{0,1:T(8,128)}, u32[]{:S(2)}) copy-start(f32[40,8]{0,1:T(8,128)} %param.17) | copy-start | bytes 3844
  287.6 1.6 copy-start.1
Sparse Core Ops, SparseCore 0:
  10.2 42.0 all-gather.4
  126.5 62.7 reduce-scatter.1
  194.7 92.9 all-reduce.2
